TPU v7x, 256 devices: a whole 4x4x8 slice. The times are simulated.
256 devices in a mesh: rows: 16 (over x, y_hi, core), mp: 16 (over y_lo, z).
Axes of the slice: x: 4, y: 4 (y_hi: 2, y_lo: 2; y = y_hi * 2 + y_lo), z: 8, core: 2. Of those that a mesh axis runs over, the one named last changes fastest.
Arguments:
- tokens: bfloat16 [2048, 3584], P('rows', 'mp'), may hold values from -6 to 6
- modality: int32 [2048], replicated, may hold values from 0 to 1, as said below
- attn_gain: float32 [2, 3584], P(None, 'mp'), may hold values from 0.1 to 1.9
- ffn_gain: float32 [2, 3584], P(None, 'mp'), may hold values from 0.1 to 1.9
- w_query: bfloat16 [2, 3584, 2048], P(None, 'mp', 'rows'), may hold values from -4 to 4
- w_keyval: bfloat16 [2, 3584, 1024], P(None, 'mp', 'rows'), may hold values from -4 to 4
- w_out: bfloat16 [2, 2048, 3584], P(None, 'rows', 'mp'), may hold values from -0.125 to 0.125
- w_gate: bfloat16 [2, 3584, 9472], P(None, 'mp', 'rows'), may hold values from -0.09375 to 0.09375
- w_up: bfloat16 [2, 3584, 9472], P(None, 'mp', 'rows'), may hold values from -0.09375 to 0.09375
- w_down: bfloat16 [2, 9472, 3584], P(None, 'rows', 'mp'), may hold values from -0.0625 to 0.0625
Outputs:
- mixed: bfloat16 [2048, 3584], P('rows', 'mp')
Inputs may be any that keep to these rules, and one draw needn't show every extreme that they name: `modality`: constant over each aligned block of 128 positions.
All inputs are finite; a program needn't handle non-finite values.
Results may differ from a plain program's by a relative error of at most 0.024.
Values may be sent and summed in bfloat16 or wider, within the bound.
A program may use at most 64 MiB of HBM per device.

v0:
```python
import jax
import jax.numpy as jnp
from jax import lax
from jax.sharding import Mesh
from jax.sharding import PartitionSpec as P

D = 3584
HD = 128
KV = 4
HEADS = 16
MODAL_BLOCK = 128
MP = ("mp_0", "mp_1")
EPSILON = 1e-06


def from_everyone(value, axis):
    copies = jnp.broadcast_to(value, (lax.axis_size(axis), *value.shape))
    return lax.all_to_all(copies, axis, split_axis=0, concat_axis=0, tiled=True)


def over_copies(value, axis):
    everything = from_everyone(value, axis)
    return jnp.sum(everything, axis=0)


def laid_out(blocks, dim):
    shape = list(blocks.shape[1:])
    shape[dim] *= blocks.shape[0]
    return jnp.moveaxis(blocks, 0, dim).reshape(shape)


def gather_directly(value, axis, dim):
    return laid_out(from_everyone(value, axis), dim)


def cut_along(value, dim, peers):
    shape = value.shape
    blocks = value.reshape(*shape[:dim], peers, shape[dim] // peers, *shape[dim + 1 :])
    return jnp.moveaxis(blocks, dim, 0)


def sent_and_summed(value, axis, dim):
    blocks = cut_along(value, dim, lax.axis_size(axis))
    arrived = lax.all_to_all(blocks, axis, split_axis=0, concat_axis=0, tiled=True)
    return arrived.astype(jnp.float32).sum(axis=0)


def reduced_to_own(blocks, axes, sequence):
    inside = blocks.shape[1:]
    blocks = blocks.reshape(*(lax.axis_size(a) for a in axes), *inside)
    blocks = jnp.moveaxis(blocks, sequence, range(len(axes))).reshape(-1, *inside)
    for k in sequence:
        blocks = lax.psum_scatter(blocks, axes[k], scatter_dimension=0, tiled=True)
    return blocks[0]


def summed_rows_2(value, axes, sequence, dim):
    peers = lax.axis_size(axes)
    return reduced_to_own(cut_along(value, dim, peers), axes, sequence)


def tower_rows(matrix, weights, tower_ids):
    per_block = matrix.shape[0] // tower_ids.shape[0]
    token_towers = jnp.repeat(tower_ids, per_block)
    is_image = (token_towers == 1)[:, None]
    nothing = jnp.zeros((), matrix.dtype)
    text_rows = jnp.where(is_image, nothing, matrix)
    image_rows = jnp.where(is_image, matrix, nothing)
    text_part = jnp.dot(text_rows, weights[0], preferred_element_type=jnp.float32)
    image_part = jnp.dot(image_rows, weights[1], preferred_element_type=jnp.float32)
    return text_part + image_part


def block_towers(modality):
    return modality.reshape(-1, MODAL_BLOCK)[:, 0]


def scaled_rows(hidden, squares, gains, token_towers):
    inverse = lax.rsqrt(squares / D + EPSILON)
    chosen = jnp.where(token_towers[:, None] == 1, gains[1][None, :], gains[0][None, :])
    return (hidden * inverse[:, None] * chosen).astype(jnp.bfloat16)


def pick_group(matrix, head_group):
    key_part = lax.dynamic_slice_in_dim(matrix, head_group * HD, HD, 1)
    value_part = lax.dynamic_slice_in_dim(matrix, KV * HD + head_group * HD, HD, 1)
    return jnp.concatenate((key_part, value_part), axis=1)


def local(tokens, modality, attn_gain, ffn_gain, w_query, w_keyval, w_out, w_gate, w_up, w_down):
    row_count = tokens.shape[0]
    total_rows = row_count * lax.axis_size("rows")
    share_rows = total_rows // lax.axis_size(MP)
    row_index = lax.axis_index("rows")
    mp_index = lax.axis_index(MP)
    own_towers = lax.dynamic_slice_in_dim(modality, row_index * row_count, row_count)
    hidden = tokens.astype(jnp.float32)
    squares = over_copies(jnp.sum(hidden * hidden, axis=1), MP)
    normed = scaled_rows(hidden, squares, attn_gain, own_towers)
    normed_all = gather_directly(normed, "rows", 0)
    joint_weight = jnp.concatenate((w_query, w_keyval), axis=2)
    picked = normed_all
    projected = sent_and_summed(
        tower_rows(picked, joint_weight, block_towers(modality)).astype(jnp.bfloat16), MP, 0
    ).astype(jnp.bfloat16)
    query_width = w_query.shape[2]
    heads_here = query_width // HD
    queries = projected[:, :query_width].reshape(share_rows, heads_here, HD)
    keyval_local = projected[:, query_width:]
    head_group = row_index * heads_here // (HEADS // KV)
    keyval_block = gather_directly(keyval_local, "rows", 1)
    keyval_all = gather_directly(pick_group(keyval_block, head_group), MP, 0)
    scores = jnp.einsum(
        "qhd,kd->hqk", queries, keyval_all[:, :HD], preferred_element_type=jnp.float32
    ) * HD ** (-0.5)
    query_pos = mp_index * share_rows + jnp.arange(share_rows, dtype=jnp.int32)
    key_pos = jnp.arange(total_rows, dtype=jnp.int32)
    allowed = key_pos[None, :] <= query_pos[:, None]
    scores = jnp.where(allowed[None, :, :], scores, -1e30)
    largest = jnp.max(scores, axis=2, keepdims=True)
    powers = jnp.exp(scores - largest)
    probs = (powers / jnp.sum(powers, axis=2, keepdims=True)).astype(jnp.bfloat16)
    context = jnp.einsum(
        "hqk,kd->qhd", probs, keyval_all[:, HD:], preferred_element_type=jnp.float32
    )
    context = context.astype(jnp.bfloat16).reshape(share_rows, query_width)
    context_all = gather_directly(context, MP, 0)
    picked = context_all
    residual = hidden + sent_and_summed(
        tower_rows(picked, w_out, block_towers(modality)).astype(jnp.bfloat16), "rows", 0
    )
    squares_ffn = over_copies(jnp.sum(residual * residual, axis=1), MP)
    normed_ffn = scaled_rows(residual, squares_ffn, ffn_gain, own_towers)
    normed_ffn_all = gather_directly(normed_ffn, "rows", 0)
    pair_weight = jnp.concatenate((w_gate, w_up), axis=2)
    hidden_width = w_gate.shape[2]
    picked = normed_ffn_all
    summed = summed_rows_2(
        tower_rows(picked, pair_weight, block_towers(modality)).astype(jnp.bfloat16), MP, (1, 0), 0
    ).astype(jnp.float32)
    activated = (jax.nn.silu(summed[:, :hidden_width]) * summed[:, hidden_width:]).astype(
        jnp.bfloat16
    )
    activated_all = lax.all_gather(activated, MP, axis=0, tiled=True)
    picked = activated_all
    mixed = residual + sent_and_summed(
        tower_rows(picked, w_down, block_towers(modality)).astype(jnp.bfloat16), "rows", 0
    )
    return mixed.astype(jnp.bfloat16)


def solution(mesh):
    torus = Mesh(mesh.devices.reshape(mesh.shape["rows"], 2, 8), ("rows", "mp_0", "mp_1"))
    in_specs = (
        P("rows", MP),
        P(),
        P(None, MP),
        P(None, MP),
        P(None, MP, "rows"),
        P(None, MP, "rows"),
        P(None, "rows", MP),
        P(None, MP, "rows"),
        P(None, MP, "rows"),
        P(None, "rows", MP),
    )
    out_specs = P("rows", MP)
    return jax.shard_map(local, mesh=torus, in_specs=in_specs, out_specs=out_specs, check_vma=False)
```

profile of v0, /device:TPU:1, one launch (start us, length us, event | category | flops | bytes accessed | tf_op | source)
XLA Modules:
  0.0 395.8 jit_solution(9332766273389813539)
XLA Ops:
  6.5 0.9 fusion.44
  8.0 10.1 %all-to-all-start = ((f32[16,1,128]{2,1,0:T(1,128)}), f32[16,1,128]{2,1,0:T(1,128)S(1)}, u32[]{:S(2)}, u32[]{:S(2)}) async-start(f32[16,1,128]{2,1,0:T(1,128)} %broadcast_in_dim.161), calls=%async_computation | async-start | bytes 16384 | tf_op jit(solution)/shard_map/all_to_all | solution.py:18
  18.2 0.8 fusion.66
  18.9 0.8 dynamic-slice_compare_fusion
  19.7 5.7 %all-to-all-done = f32[16,1,128]{2,1,0:T(1,128)S(1)} async-done(((f32[16,1,128]{2,1,0:T(1,128)}), f32[16,1,128]{2,1,0:T(1,128)S(1)}, u32[]{:S(2)}, u32[]{:S(2)}) %all-to-all-start) | async-done | bytes 8224 | tf_op jit(solution)/shard_map/all_to_all | solution.py:18
  25.5 0.9 fusion.46
  26.4 1.1 broadcast_in_dim.167
  27.5 8.8 %all-to-all-start.1 = ((bf16[16,128,224]{1,2,0:T(8,128)(2,1)}), bf16[16,128,224]{1,2,0:T(8,128)(2,1)S(1)}, u32[]{:S(2)}, u32[]{:S(2)}) async-start(bf16[16,128,224]{1,2,0:T(8,128)(2,1)} %broadcast_in_dim.167), calls=%async_computation.1 | async-start | bytes 1835008 | tf_op jit(solution)/shard_map/all_to_all | solution.py:18
  36.5 15.1 %all-to-all-done.1 = bf16[16,128,224]{1,2,0:T(8,128)(2,1)S(1)} async-done(((bf16[16,128,224]{1,2,0:T(8,128)(2,1)}), bf16[16,128,224]{1,2,0:T(8,128)(2,1)S(1)}, u32[]{:S(2)}, u32[]{:S(2)}) %all-to-all-start.1) | async-done | bytes 917536 | tf_op jit(solution)/shard_map/all_to_all | solution.py:18
  52.8 22.3 %all_to_all.52 = bf16[16,128,192]{1,2,0:T(8,128)(2,1)S(1)} all-to-all(bf16[16,128,192]{1,2,0:T(8,128)(2,1)S(1)} %bitcast.107), channel_id=1, replica_groups=mesh['rows'=16,'mp_0'=2,'mp_1'=8] {'mp_0','mp_1'}, dimensions={0} | all-to-all | bytes 1572864 | tf_op jit(solution)/shard_map/all_to_all | solution.py:44
  76.0 6.5 %all-to-all-start.3 = ((bf16[16,128,64]{1,2,0:T(8,128)(2,1)}), bf16[16,128,64]{1,2,0:T(8,128)(2,1)S(1)}, u32[]{:S(2)}, u32[]{:S(2)}) async-start(bf16[16,128,64]{1,2,0:T(8,128)(2,1)} %broadcast_in_dim.168), calls=%async_computation.3 | async-start | bytes 524288 | tf_op jit(solution)/shard_map/all_to_all | solution.py:18
  82.5 8.9 %all-to-all-done.3 = bf16[16,128,64]{1,2,0:T(8,128)(2,1)S(1)} async-done(((bf16[16,128,64]{1,2,0:T(8,128)(2,1)}), bf16[16,128,64]{1,2,0:T(8,128)(2,1)S(1)}, u32[]{:S(2)}, u32[]{:S(2)}) %all-to-all-start.3) | async-done | bytes 262176 | tf_op jit(solution)/shard_map/all_to_all | solution.py:18
  91.5 1.1 broadcast_in_dim.169
  92.5 4.1 %all-to-all-start.4 = ((bf16[16,128,256]{2,1,0:T(8,128)(2,1)}), bf16[16,128,256]{2,1,0:T(8,128)(2,1)S(1)}, u32[]{:S(2)}, u32[]{:S(2)}) async-start(bf16[16,128,256]{2,1,0:T(8,128)(2,1)} %broadcast_in_dim.169), calls=%async_computation.4 | async-start | bytes 2097152 | tf_op jit(solution)/shard_map/all_to_all | solution.py:18
  96.7 25.6 %all-to-all-done.4 = bf16[16,128,256]{2,1,0:T(8,128)(2,1)S(1)} async-done(((bf16[16,128,256]{2,1,0:T(8,128)(2,1)}), bf16[16,128,256]{2,1,0:T(8,128)(2,1)S(1)}, u32[]{:S(2)}, u32[]{:S(2)}) %all-to-all-start.4) | async-done | bytes 1048608 | tf_op jit(solution)/shard_map/all_to_all | solution.py:18
  123.6 19.5 %all_to_all.53 = bf16[16,128,128]{2,1,0:T(8,128)(2,1)S(1)} all-to-all(bf16[16,128,128]{2,1,0:T(8,128)(2,1)S(1)} %broadcast_in_dim.171), channel_id=1, replica_groups=mesh['rows'=16,'mp_0'=2,'mp_1'=8] {'mp_0','mp_1'}, dimensions={0} | all-to-all | bytes 1048576 | tf_op jit(solution)/shard_map/all_to_all | solution.py:18
  144.3 21.5 %all_to_all.54 = bf16[16,128,224]{1,2,0:T(8,128)(2,1)S(1)} all-to-all(bf16[16,128,224]{1,2,0:T(8,128)(2,1)S(1)} %bitcast.105), channel_id=1, replica_groups=mesh['rows'=16,'mp_0'=2,'mp_1'=8] {'rows'}, dimensions={0} | all-to-all | bytes 1835008 | tf_op jit(solution)/shard_map/all_to_all | solution.py:44
  166.6 4.2 %all-to-all-start.7 = ((f32[16,1,128]{2,1,0:T(1,128)}), f32[16,1,128]{2,1,0:T(1,128)S(1)}, u32[]{:S(2)}, u32[]{:S(2)}) async-start(f32[16,1,128]{2,1,0:T(1,128)} %broadcast_in_dim.175), calls=%async_computation.7 | async-start | bytes 16384 | tf_op jit(solution)/shard_map/all_to_all | solution.py:18
  170.8 7.2 %all-to-all-done.7 = f32[16,1,128]{2,1,0:T(1,128)S(1)} async-done(((f32[16,1,128]{2,1,0:T(1,128)}), f32[16,1,128]{2,1,0:T(1,128)S(1)}, u32[]{:S(2)}, u32[]{:S(2)}) %all-to-all-start.7) | async-done | bytes 8224 | tf_op jit(solution)/shard_map/all_to_all | solution.py:18
  178.3 20.8 %all_to_all.55 = bf16[16,128,224]{1,2,0:T(8,128)(2,1)S(1)} all-to-all(bf16[16,128,224]{1,2,0:T(8,128)(2,1)S(1)} %broadcast_in_dim.180), channel_id=1, replica_groups=mesh['rows'=16,'mp_0'=2,'mp_1'=8] {'rows'}, dimensions={0} | all-to-all | bytes 1835008 | tf_op jit(solution)/shard_map/all_to_all | solution.py:18
  199.3 0.9 copy-done
  200.3 1.7 fusion.22
  202.0 1.8 fusion.10
  203.7 1.6 copy.76
  205.4 3.4 copy.67
  208.9 53.6 %reduce-scatter.3.cloned.1.call-done = bf16[2,128,1184]{1,2,0:T(8,128)(2,1)} async-done(((bf16[16,128,1184]{1,2,0:T(8,128)(2,1)}), bf16[2,128,1184]{1,2,0:T(8,128)(2,1)}) %reduce-scatter.3.cloned.1.call-update) | async-done | bytes 606224 | tf_op jit(solution)/shard_map/reduce_scatter | solution.py:53
  262.5 21.6 %reduce-scatter.5.cloned.1.call-done = bf16[1,128,1184]{1,2,0:T(8,128)(2,1)} async-done(((bf16[2,128,1184]{1,2,0:T(8,128)(2,1)}), bf16[1,128,1184]{1,2,0:T(8,128)(2,1)}) %reduce-scatter.5.cloned.1.call-update) | async-done | bytes 303120 | tf_op jit(solution)/shard_map/reduce_scatter | solution.py:53
  284.2 1.0 bitcast_convert_fusion
  286.0 64.7 %all-gather.2.cloned.1.call-done = bf16[2048,592]{0,1:T(8,128)(2,1)} async-done(((bf16[128,592]{0,1:T(8,128)(2,1)}), bf16[2048,592]{0,1:T(8,128)(2,1)}) %all-gather.2.cloned.1.call-update) | async-done | bytes 2424848 | tf_op jit(solution)/shard_map/all_gather | solution.py:144
  350.8 2.7 fusion.5
  353.5 0.9 fusion.12
  354.6 33.9 %all_to_all.56 = bf16[16,128,224]{1,2,0:T(8,128)(2,1)S(1)} all-to-all(bf16[16,128,224]{1,2,0:T(8,128)(2,1)S(1)} %bitcast.106), channel_id=1, replica_groups=mesh['rows'=16,'mp_0'=2,'mp_1'=8] {'rows'}, dimensions={0} | all-to-all | bytes 1835008 | tf_op jit(solution)/shard_map/all_to_all | solution.py:44
  (64 shorter events, 8.8 us)
Async XLA Ops:
  6.5 29.8 %copy-start.6 = (s32[2048]{0:T(1024)S(1)}, s32[2048]{0:T(1024)}, u32[]{:S(2)}) copy-start(s32[2048]{0:T(1024)} %param.11) | copy-start | bytes 24580
  6.5 29.7 %copy-start.5 = (bf16[2,224,64]{1,2,0:T(8,128)(2,1)S(1)}, bf16[2,224,64]{1,2,0:T(8,128)(2,1)}, u32[]{:S(2)}) copy-start(bf16[2,224,64]{1,2,0:T(8,128)(2,1)} %param.15) | copy-start | bytes 172036
  8.0 17.4 %all-to-all-start = ((f32[16,1,128]{2,1,0:T(1,128)}), f32[16,1,128]{2,1,0:T(1,128)S(1)}, u32[]{:S(2)}, u32[]{:S(2)}) async-start(f32[16,1,128]{2,1,0:T(1,128)} %broadcast_in_dim.161), calls=%async_computation | async-start | bytes 16384 | tf_op jit(solution)/shard_map/all_to_all | solution.py:18
  27.5 24.1 %all-to-all-start.1 = ((bf16[16,128,224]{1,2,0:T(8,128)(2,1)}), bf16[16,128,224]{1,2,0:T(8,128)(2,1)S(1)}, u32[]{:S(2)}, u32[]{:S(2)}) async-start(bf16[16,128,224]{1,2,0:T(8,128)(2,1)} %broadcast_in_dim.167), calls=%async_computation.1 | async-start | bytes 1835008 | tf_op jit(solution)/shard_map/all_to_all | solution.py:18
  36.2 15.6 %copy-start.3 = (bf16[2,224,128]{2,1,0:T(8,128)(2,1)S(1)}, bf16[2,224,128]{2,1,0:T(8,128)(2,1)}, u32[]{:S(2)}) copy-start(bf16[2,224,128]{2,1,0:T(8,128)(2,1)} %param.14) | copy-start | bytes 344068
  76.0 15.3 %all-to-all-start.3 = ((bf16[16,128,64]{1,2,0:T(8,128)(2,1)}), bf16[16,128,64]{1,2,0:T(8,128)(2,1)S(1)}, u32[]{:S(2)}, u32[]{:S(2)}) async-start(bf16[16,128,64]{1,2,0:T(8,128)(2,1)} %broadcast_in_dim.168), calls=%async_computation.3 | async-start | bytes 524288 | tf_op jit(solution)/shard_map/all_to_all | solution.py:18
  92.5 29.7 %all-to-all-start.4 = ((bf16[16,128,256]{2,1,0:T(8,128)(2,1)}), bf16[16,128,256]{2,1,0:T(8,128)(2,1)S(1)}, u32[]{:S(2)}, u32[]{:S(2)}) async-start(bf16[16,128,256]{2,1,0:T(8,128)(2,1)} %broadcast_in_dim.169), calls=%async_computation.4 | async-start | bytes 2097152 | tf_op jit(solution)/shard_map/all_to_all | solution.py:18
  123.4 19.9 %copy-start.4 = (bf16[2,128,224]{1,2,0:T(8,128)(2,1)S(1)}, bf16[2,128,224]{1,2,0:T(8,128)(2,1)}, u32[]{:S(2)}) copy-start(bf16[2,128,224]{1,2,0:T(8,128)(2,1)} %param.16) | copy-start | bytes 344068
  144.3 21.6 %copy-start.2 = (bf16[128,224]{0,1:T(8,128)(2,1)S(1)}, bf16[128,224]{0,1:T(8,128)(2,1)}, u32[]{:S(2)}) copy-start(bf16[128,224]{0,1:T(8,128)(2,1)} %param.10) | copy-start | bytes 172036
  144.3 26.5 %copy-start.7 = (f32[2,224]{1,0:T(2,128)S(1)}, f32[2,224]{1,0:T(2,128)}, u32[]{:S(2)}) copy-start(f32[2,224]{1,0:T(2,128)} %param.13) | copy-start | bytes 5380
  166.6 11.4 %all-to-all-start.7 = ((f32[16,1,128]{2,1,0:T(1,128)}), f32[16,1,128]{2,1,0:T(1,128)S(1)}, u32[]{:S(2)}, u32[]{:S(2)}) async-start(f32[16,1,128]{2,1,0:T(1,128)} %broadcast_in_dim.175), calls=%async_computation.7 | async-start | bytes 16384 | tf_op jit(solution)/shard_map/all_to_all | solution.py:18
  170.7 91.8 %reduce-scatter.3.cloned.1.call-start = ((), (), s32[]{:S(2)}) async-start(), calls=%async_computation.12 | async-start | bytes 5455872 | tf_op jit(solution)/shard_map/reduce_scatter | solution.py:53
  199.1 1.1 copy-start
  199.1 1.2 copy-start.1
  208.8 142.0 %copy-start.9 = (bf16[2,592,224]{1,2,0:T(8,128)(2,1)S(1)}, bf16[2,592,224]{1,2,0:T(8,128)(2,1)}, u32[]{:S(2)}) copy-start(bf16[2,592,224]{1,2,0:T(8,128)(2,1)} %param.19) | copy-start | bytes 1591300
  208.8 75.4 %reduce-scatter.5.cloned.1.call-start = ((), (), s32[]{:S(2)}) async-start(), calls=%async_computation.13 | async-start | bytes 909312 | tf_op jit(solution)/shard_map/reduce_scatter | solution.py:53
  262.5 88.3 %all-gather.2.cloned.1.call-start = ((), (), s32[]{:S(2)}) async-start(), calls=%async_computation.14 | async-start | bytes 2576384 | tf_op jit(solution)/shard_map/all_gather | solution.py:144
  350.8 2.7 copy-start.8
Sparse Core Ops, SparseCore 0:
  208.9 53.5 reduce-scatter.2
  265.0 19.1 reduce-scatter.4
  286.1 64.6 all-gather.1
where the time goes:
time: 397 us; the launch traced here: 396 us
  waiting for transfers between devices  202 us (51%)
  blocking collectives  118 us (30%)
  starting transfers between devices  33.8 us (9%)
  between operations  13.4 us (3%)
  local copies, waits for them, and re-layouts  12.1 us (3%)
  matrix products  9.47 us (2%)
  other arithmetic  6.53 us (2%)
    all_to_all x3, blocking collectives, sent_and_summed(): lax.all_to_all(blocks, axis, split_axis=0, concat_axis=0, tiled=True)  77.6 us
    reduce_scatter x2, waiting for transfers between devices, reduced_to_own(): blocks = lax.psum_scatter(blocks, axes[k], scatter_dimension=0, tiled=True)  75.2 us
    all_gather x1, waiting for transfers between devices, local(): activated_all = lax.all_gather(activated, MP, axis=0, tiled=True)  64.7 us
    all_to_all x5, waiting for transfers between devices, from_everyone(): return lax.all_to_all(copies, axis, split_axis=0, concat_axis=0, tiled=True)  62.4 us
    all_to_all x2, blocking collectives, from_everyone(): return lax.all_to_all(copies, axis, split_axis=0, concat_axis=0, tiled=True)  40.3 us
    all_to_all x5, starting transfers between devices, from_everyone(): return lax.all_to_all(copies, axis, split_axis=0, concat_axis=0, tiled=True)  33.6 us
  transfers between devices with their start and end apart: 8, of which 8 were waited for; matrix products, arithmetic and copies ran while one was open for 0% of the time, Pallas kernels for 0%

commit v1 on v0

--- a/solution.py
+++ b/solution.py
@@ -141,7 +141,8 @@
     activated = (jax.nn.silu(summed[:, :hidden_width]) * summed[:, hidden_width:]).astype(
         jnp.bfloat16
     )
-    activated_all = lax.all_gather(activated, MP, axis=0, tiled=True)
+    sent = jnp.stack([activated] * lax.axis_size(MP))
+    activated_all = jnp.concatenate(lax.all_to_all(sent, MP, 0, 0), axis=0)
     picked = activated_all
     mixed = residual + sent_and_summed(
         tower_rows(picked, w_down, block_towers(modality)).astype(jnp.bfloat16), "rows", 0

time: 397 us -> 383 us (0.965)
  waiting for transfers between devices: 202 us -> 138 us
  blocking collectives: 118 us -> 170 us
    all_gather x1 -> x0, waiting for transfers between devices: 64.7 us -> none  [local(): activated_all = lax.all_gather(activated, MP, axis=0, tiled=True)]
    all_to_all x0 -> x1, blocking collectives: none -> 61.2 us  [local(): activated_all = jnp.concatenate(lax.all_to_all(sent, MP, 0, 0), axis=0)]
    all_to_all x3, blocking collectives: 77.6 us -> 68.6 us  [sent_and_summed(): lax.all_to_all(blocks, axis, split_axis=0, concat_axis=0, tiled=True)]
  transfers between devices with their start and end apart: 8 -> 7, of which waited for: 8 -> 7; matrix products, arithmetic and copies ran while one was open for 0% -> 0% of each run, Pallas kernels for 0% -> 0%
where the time goes in v1:
time: 383 us; the launch traced here: 382 us
  blocking collectives  170 us (44%)
  waiting for transfers between devices  138 us (36%)
  starting transfers between devices  33.7 us (9%)
  between operations  13.7 us (4%)
  local copies, waits for them, and re-layouts  13 us (3%)
  matrix products  7.66 us (2%)
  other arithmetic  6.26 us (2%)
    reduce_scatter x2, waiting for transfers between devices, reduced_to_own(): blocks = lax.psum_scatter(blocks, axes[k], scatter_dimension=0, tiled=True)  75.3 us
    all_to_all x3, blocking collectives, sent_and_summed(): lax.all_to_all(blocks, axis, split_axis=0, concat_axis=0, tiled=True)  68.6 us
    all_to_all x5, waiting for transfers between devices, from_everyone(): return lax.all_to_all(copies, axis, split_axis=0, concat_axis=0, tiled=True)  62.4 us
    all_to_all x1, blocking collectives, local(): activated_all = jnp.concatenate(lax.all_to_all(sent, MP, 0, 0), axis=0)  61.2 us
    all_to_all x2, blocking collectives, from_everyone(): return lax.all_to_all(copies, axis, split_axis=0, concat_axis=0, tiled=True)  40.3 us
    all_to_all x5, starting transfers between devices, from_everyone(): return lax.all_to_all(copies, axis, split_axis=0, concat_axis=0, tiled=True)  33.7 us
  transfers between devices with their start and end apart: 7, of which 7 were waited for; matrix products, arithmetic and copies ran while one was open for 0% of the time, Pallas kernels for 0%

profile of v1, /device:TPU:1, one launch (start us, length us, event | category | flops | bytes accessed | tf_op | source)
XLA Modules:
  0.0 382.4 jit_solution(16232265211774221261)
XLA Ops:
  6.5 0.9 fusion.42
  8.0 10.1 %all-to-all-start = ((f32[16,1,128]{2,1,0:T(1,128)}), f32[16,1,128]{2,1,0:T(1,128)S(1)}, u32[]{:S(2)}, u32[]{:S(2)}) async-start(f32[16,1,128]{2,1,0:T(1,128)} %broadcast_in_dim.159), calls=%async_computation | async-start | bytes 16384 | tf_op jit(solution)/shard_map/all_to_all | solution.py:18
  18.2 0.8 fusion.62
  18.9 0.8 dynamic-slice_compare_fusion
  19.7 5.7 %all-to-all-done = f32[16,1,128]{2,1,0:T(1,128)S(1)} async-done(((f32[16,1,128]{2,1,0:T(1,128)}), f32[16,1,128]{2,1,0:T(1,128)S(1)}, u32[]{:S(2)}, u32[]{:S(2)}) %all-to-all-start) | async-done | bytes 8224 | tf_op jit(solution)/shard_map/all_to_all | solution.py:18
  25.5 0.9 fusion.44
  26.4 1.0 broadcast_in_dim.165
  27.5 8.8 %all-to-all-start.1 = ((bf16[16,128,224]{1,2,0:T(8,128)(2,1)}), bf16[16,128,224]{1,2,0:T(8,128)(2,1)S(1)}, u32[]{:S(2)}, u32[]{:S(2)}) async-start(bf16[16,128,224]{1,2,0:T(8,128)(2,1)} %broadcast_in_dim.165), calls=%async_computation.1 | async-start | bytes 1835008 | tf_op jit(solution)/shard_map/all_to_all | solution.py:18
  36.5 15.1 %all-to-all-done.1 = bf16[16,128,224]{1,2,0:T(8,128)(2,1)S(1)} async-done(((bf16[16,128,224]{1,2,0:T(8,128)(2,1)}), bf16[16,128,224]{1,2,0:T(8,128)(2,1)S(1)}, u32[]{:S(2)}, u32[]{:S(2)}) %all-to-all-start.1) | async-done | bytes 917536 | tf_op jit(solution)/shard_map/all_to_all | solution.py:18
  52.8 22.3 %all_to_all.57 = bf16[16,128,192]{1,2,0:T(8,128)(2,1)S(1)} all-to-all(bf16[16,128,192]{1,2,0:T(8,128)(2,1)S(1)} %bitcast.117), channel_id=1, replica_groups=mesh['rows'=16,'mp_0'=2,'mp_1'=8] {'mp_0','mp_1'}, dimensions={0} | all-to-all | bytes 1572864 | tf_op jit(solution)/shard_map/all_to_all | solution.py:44
  76.0 6.5 %all-to-all-start.3 = ((bf16[16,128,64]{1,2,0:T(8,128)(2,1)}), bf16[16,128,64]{1,2,0:T(8,128)(2,1)S(1)}, u32[]{:S(2)}, u32[]{:S(2)}) async-start(bf16[16,128,64]{1,2,0:T(8,128)(2,1)} %broadcast_in_dim.166), calls=%async_computation.3 | async-start | bytes 524288 | tf_op jit(solution)/shard_map/all_to_all | solution.py:18
  82.5 8.9 %all-to-all-done.3 = bf16[16,128,64]{1,2,0:T(8,128)(2,1)S(1)} async-done(((bf16[16,128,64]{1,2,0:T(8,128)(2,1)}), bf16[16,128,64]{1,2,0:T(8,128)(2,1)S(1)}, u32[]{:S(2)}, u32[]{:S(2)}) %all-to-all-start.3) | async-done | bytes 262176 | tf_op jit(solution)/shard_map/all_to_all | solution.py:18
  91.5 1.1 broadcast_in_dim.167
  92.6 4.1 %all-to-all-start.4 = ((bf16[16,128,256]{2,1,0:T(8,128)(2,1)}), bf16[16,128,256]{2,1,0:T(8,128)(2,1)S(1)}, u32[]{:S(2)}, u32[]{:S(2)}) async-start(bf16[16,128,256]{2,1,0:T(8,128)(2,1)} %broadcast_in_dim.167), calls=%async_computation.4 | async-start | bytes 2097152 | tf_op jit(solution)/shard_map/all_to_all | solution.py:18
  96.7 25.6 %all-to-all-done.4 = bf16[16,128,256]{2,1,0:T(8,128)(2,1)S(1)} async-done(((bf16[16,128,256]{2,1,0:T(8,128)(2,1)}), bf16[16,128,256]{2,1,0:T(8,128)(2,1)S(1)}, u32[]{:S(2)}, u32[]{:S(2)}) %all-to-all-start.4) | async-done | bytes 1048608 | tf_op jit(solution)/shard_map/all_to_all | solution.py:18
  123.6 19.5 %all_to_all.58 = bf16[16,128,128]{2,1,0:T(8,128)(2,1)S(1)} all-to-all(bf16[16,128,128]{2,1,0:T(8,128)(2,1)S(1)} %broadcast_in_dim.169), channel_id=1, replica_groups=mesh['rows'=16,'mp_0'=2,'mp_1'=8] {'mp_0','mp_1'}, dimensions={0} | all-to-all | bytes 1048576 | tf_op jit(solution)/shard_map/all_to_all | solution.py:18
  144.3 21.5 %all_to_all.59 = bf16[16,128,224]{1,2,0:T(8,128)(2,1)S(1)} all-to-all(bf16[16,128,224]{1,2,0:T(8,128)(2,1)S(1)} %bitcast.115), channel_id=1, replica_groups=mesh['rows'=16,'mp_0'=2,'mp_1'=8] {'rows'}, dimensions={0} | all-to-all | bytes 1835008 | tf_op jit(solution)/shard_map/all_to_all | solution.py:44
  166.6 4.2 %all-to-all-start.7 = ((f32[16,1,128]{2,1,0:T(1,128)}), f32[16,1,128]{2,1,0:T(1,128)S(1)}, u32[]{:S(2)}, u32[]{:S(2)}) async-start(f32[16,1,128]{2,1,0:T(1,128)} %broadcast_in_dim.172), calls=%async_computation.7 | async-start | bytes 16384 | tf_op jit(solution)/shard_map/all_to_all | solution.py:18
  170.8 7.2 %all-to-all-done.7 = f32[16,1,128]{2,1,0:T(1,128)S(1)} async-done(((f32[16,1,128]{2,1,0:T(1,128)}), f32[16,1,128]{2,1,0:T(1,128)S(1)}, u32[]{:S(2)}, u32[]{:S(2)}) %all-to-all-start.7) | async-done | bytes 8224 | tf_op jit(solution)/shard_map/all_to_all | solution.py:18
  178.3 20.8 %all_to_all.60 = bf16[16,128,224]{1,2,0:T(8,128)(2,1)S(1)} all-to-all(bf16[16,128,224]{1,2,0:T(8,128)(2,1)S(1)} %broadcast_in_dim.177), channel_id=1, replica_groups=mesh['rows'=16,'mp_0'=2,'mp_1'=8] {'rows'}, dimensions={0} | all-to-all | bytes 1835008 | tf_op jit(solution)/shard_map/all_to_all | solution.py:18
  199.3 0.9 copy-done
  200.3 1.7 fusion.20
  202.0 1.8 fusion.10
  203.8 1.6 copy.86
  205.4 3.4 copy.73
  208.9 53.6 %reduce-scatter.3.cloned.1.call-done = bf16[2,128,1184]{1,2,0:T(8,128)(2,1)} async-done(((bf16[16,128,1184]{1,2,0:T(8,128)(2,1)}), bf16[2,128,1184]{1,2,0:T(8,128)(2,1)}) %reduce-scatter.3.cloned.1.call-update) | async-done | bytes 606224 | tf_op jit(solution)/shard_map/reduce_scatter | solution.py:53
  262.5 21.7 %reduce-scatter.5.cloned.1.call-done = bf16[1,128,1184]{1,2,0:T(8,128)(2,1)} async-done(((bf16[2,128,1184]{1,2,0:T(8,128)(2,1)}), bf16[1,128,1184]{1,2,0:T(8,128)(2,1)}) %reduce-scatter.5.cloned.1.call-update) | async-done | bytes 303120 | tf_op jit(solution)/shard_map/reduce_scatter | solution.py:53
  284.2 1.0 bitcast_convert_fusion
  285.6 61.2 %all_to_all.61 = bf16[16,128,592]{1,2,0:T(8,128)(2,1)S(1)} all-to-all(bf16[16,128,592]{1,2,0:T(8,128)(2,1)S(1)} %stack.2), channel_id=1, replica_groups=mesh['rows'=16,'mp_0'=2,'mp_1'=8] {'mp_0','mp_1'}, dimensions={0} | all-to-all | bytes 4849664 | tf_op jit(solution)/shard_map/all_to_all | solution.py:145
  347.9 0.9 fusion.6
  348.8 0.9 fusion.11
  349.9 24.9 %all_to_all.62 = bf16[16,128,224]{1,2,0:T(8,128)(2,1)S(1)} all-to-all(bf16[16,128,224]{1,2,0:T(8,128)(2,1)S(1)} %bitcast.116), channel_id=1, replica_groups=mesh['rows'=16,'mp_0'=2,'mp_1'=8] {'rows'}, dimensions={0} | all-to-all | bytes 1835008 | tf_op jit(solution)/shard_map/all_to_all | solution.py:44
  (61 shorter events, 9.4 us)
Async XLA Ops:
  6.5 29.8 %copy-start.7 = (s32[2048]{0:T(1024)S(1)}, s32[2048]{0:T(1024)}, u32[]{:S(2)}) copy-start(s32[2048]{0:T(1024)} %param.11) | copy-start | bytes 24580
  6.5 29.7 %copy-start.6 = (bf16[2,224,64]{1,2,0:T(8,128)(2,1)S(1)}, bf16[2,224,64]{1,2,0:T(8,128)(2,1)}, u32[]{:S(2)}) copy-start(bf16[2,224,64]{1,2,0:T(8,128)(2,1)} %param.15) | copy-start | bytes 172036
  8.0 17.4 %all-to-all-start = ((f32[16,1,128]{2,1,0:T(1,128)}), f32[16,1,128]{2,1,0:T(1,128)S(1)}, u32[]{:S(2)}, u32[]{:S(2)}) async-start(f32[16,1,128]{2,1,0:T(1,128)} %broadcast_in_dim.159), calls=%async_computation | async-start | bytes 16384 | tf_op jit(solution)/shard_map/all_to_all | solution.py:18
  27.5 24.1 %all-to-all-start.1 = ((bf16[16,128,224]{1,2,0:T(8,128)(2,1)}), bf16[16,128,224]{1,2,0:T(8,128)(2,1)S(1)}, u32[]{:S(2)}, u32[]{:S(2)}) async-start(bf16[16,128,224]{1,2,0:T(8,128)(2,1)} %broadcast_in_dim.165), calls=%async_computation.1 | async-start | bytes 1835008 | tf_op jit(solution)/shard_map/all_to_all | solution.py:18
  36.2 15.6 %copy-start.4 = (bf16[2,224,128]{2,1,0:T(8,128)(2,1)S(1)}, bf16[2,224,128]{2,1,0:T(8,128)(2,1)}, u32[]{:S(2)}) copy-start(bf16[2,224,128]{2,1,0:T(8,128)(2,1)} %param.14) | copy-start | bytes 344068
  76.0 15.4 %all-to-all-start.3 = ((bf16[16,128,64]{1,2,0:T(8,128)(2,1)}), bf16[16,128,64]{1,2,0:T(8,128)(2,1)S(1)}, u32[]{:S(2)}, u32[]{:S(2)}) async-start(bf16[16,128,64]{1,2,0:T(8,128)(2,1)} %broadcast_in_dim.166), calls=%async_computation.3 | async-start | bytes 524288 | tf_op jit(solution)/shard_map/all_to_all | solution.py:18
  92.6 29.7 %all-to-all-start.4 = ((bf16[16,128,256]{2,1,0:T(8,128)(2,1)}), bf16[16,128,256]{2,1,0:T(8,128)(2,1)S(1)}, u32[]{:S(2)}, u32[]{:S(2)}) async-start(bf16[16,128,256]{2,1,0:T(8,128)(2,1)} %broadcast_in_dim.167), calls=%async_computation.4 | async-start | bytes 2097152 | tf_op jit(solution)/shard_map/all_to_all | solution.py:18
  123.4 19.9 %copy-start.5 = (bf16[2,128,224]{1,2,0:T(8,128)(2,1)S(1)}, bf16[2,128,224]{1,2,0:T(8,128)(2,1)}, u32[]{:S(2)}) copy-start(bf16[2,128,224]{1,2,0:T(8,128)(2,1)} %param.16) | copy-start | bytes 344068
  144.3 21.6 %copy-start.2 = (bf16[128,224]{0,1:T(8,128)(2,1)S(1)}, bf16[128,224]{0,1:T(8,128)(2,1)}, u32[]{:S(2)}) copy-start(bf16[128,224]{0,1:T(8,128)(2,1)} %param.10) | copy-start | bytes 172036
  144.3 26.5 %copy-start.8 = (f32[2,224]{1,0:T(2,128)S(1)}, f32[2,224]{1,0:T(2,128)}, u32[]{:S(2)}) copy-start(f32[2,224]{1,0:T(2,128)} %param.13) | copy-start | bytes 5380
  166.6 11.4 %all-to-all-start.7 = ((f32[16,1,128]{2,1,0:T(1,128)}), f32[16,1,128]{2,1,0:T(1,128)S(1)}, u32[]{:S(2)}, u32[]{:S(2)}) async-start(f32[16,1,128]{2,1,0:T(1,128)} %broadcast_in_dim.172), calls=%async_computation.7 | async-start | bytes 16384 | tf_op jit(solution)/shard_map/all_to_all | solution.py:18
  170.7 91.8 %reduce-scatter.3.cloned.1.call-start = ((), (), s32[]{:S(2)}) async-start(), calls=%async_computation.13 | async-start | bytes 5455872 | tf_op jit(solution)/shard_map/reduce_scatter | solution.py:53
  199.1 1.1 copy-start
  199.1 1.2 copy-start.1
  208.8 75.4 %reduce-scatter.5.cloned.1.call-start = ((), (), s32[]{:S(2)}) async-start(), calls=%async_computation.14 | async-start | bytes 909312 | tf_op jit(solution)/shard_map/reduce_scatter | solution.py:53
  346.9 1.1 copy-start.3
Sparse Core Ops, SparseCore 0:
  208.9 53.5 reduce-scatter.2
  265.0 19.1 reduce-scatter.4
